TPU v7x, 32 devices: a whole 2x2x4 slice. The times are simulated.
32 devices in a mesh: img: 4 (over y, core), proj: 8 (over z, x).
Axes of the slice: x: 2, y: 2, z: 4, core: 2. Of those that a mesh axis runs over, the one named last changes fastest.
Arguments:
- images: bfloat16 [512, 4096], P('img'), may hold values from -48 to 48
- projections: bfloat16 [2560, 4096], P('proj'), may hold values from -6 to 6
- noise_weight: float32 [4096], replicated, may hold values from 0.02 to 0.08
- defocus: float32 [512], P('img'), may hold values from 2 to 8
- orient_count: int32 [512], P('img'), may hold values from 160 to 2560, as said below
- term_limit: int32 [512], P('img'), may hold values from 2048 to 4096
- block_plan: int32 [16], replicated, may hold values from 0 to 15, each once
Outputs:
- reconstruction: bfloat16 [2560, 4096], P('proj', 'img')
- evidence_next: float32 [512], P('img')
Inputs may be any that keep to these rules, and one draw needn't show every extreme that they name: Orientations 0 to orient_count[i] - 1 are the significant ones of image i; some image has all 2560.
All inputs are finite; a program needn't handle non-finite values.
Results may differ from a plain program's by a relative error of at most 0.018.
Values may be sent and summed in bfloat16 or wider, within the bound.
A program may use at most 64 MiB of HBM per device.

v0:
```python
import math

import jax
import jax.numpy as jnp
from jax import lax
from jax.sharding import PartitionSpec as P

F = 4096
BLOCK = 32


def contrast_table(defocus, width):
    frequency = (jnp.arange(width, dtype=jnp.float32) + 1.0) / width
    return jnp.sin(2.0 * math.pi * defocus[:, None] * frequency[None, :] + 0.1)


def image_terms(pixels, noise_weight, defocus, limits):
    width = pixels.shape[1]
    contrast = contrast_table(defocus, width)
    keep_mask = (jnp.arange(width, dtype=jnp.int32)[None, :] < limits[:, None]).astype(jnp.float32)
    values = pixels.astype(jnp.float32)
    weighted = (keep_mask * noise_weight[None, :] * contrast * values).astype(jnp.bfloat16)
    weighted_sq = (keep_mask * noise_weight[None, :] * contrast * contrast).astype(jnp.bfloat16)
    back_images = (keep_mask * contrast * values).astype(jnp.bfloat16)
    return (weighted, weighted_sq, back_images)


def slice_weight_sums(every_post, focus_all, limit_all, start, slice_width, img_count, img_rows):
    term_ids = jnp.arange(slice_width, dtype=jnp.int32) + start
    term_float = term_ids.astype(jnp.float32)
    frequency = (term_float + 1.0) / F
    contrast = jnp.sin(2.0 * math.pi * focus_all[:, None] * frequency[None, :] + 0.1)
    keep_mask = (term_float[None, :] < limit_all[:, None]).astype(jnp.float32)
    rebuilt = (keep_mask * contrast * contrast).astype(jnp.bfloat16)
    rebuilt = rebuilt.reshape(img_count, img_rows, slice_width)
    partial_value = jnp.einsum(
        "jbi,bif->bjf", every_post, rebuilt, preferred_element_type=jnp.float32
    )
    partial_value = lax.optimization_barrier(partial_value.astype(jnp.bfloat16)).astype(jnp.float32)
    return jnp.sum(partial_value, axis=0)


def shards(images, projections, noise_weight, defocus, orient_count, term_limit, block_plan):
    proj_rows = projections.shape[0]
    img_rows = images.shape[0]
    weighted, weighted_sq, back_images = image_terms(images, noise_weight, defocus, term_limit)
    proj_sq = (projections.astype(jnp.float32) * projections.astype(jnp.float32)).astype(
        jnp.bfloat16
    )
    contract = (((1,), (1,)), ((), ()))
    scores = lax.dot_general(projections, weighted, contract, preferred_element_type=jnp.float32)
    scores = scores - 0.5 * lax.dot_general(
        proj_sq, weighted_sq, contract, preferred_element_type=jnp.float32
    )
    orient_ids = lax.axis_index("proj") * proj_rows + jnp.arange(proj_rows, dtype=jnp.int32)
    significant = orient_ids[:, None] < orient_count[None, :]
    local_peak = jnp.max(jnp.where(significant, scores, -1e30), axis=0)
    row_peak = lax.pmax(local_peak, "proj")
    safe = jnp.where(significant, scores, row_peak[None, :])
    local_mass = jnp.sum(jnp.where(significant, jnp.exp(safe - row_peak[None, :]), 0.0), axis=0)
    row_mass = lax.psum(local_mass, "proj")
    log_evidence = row_peak + jnp.log(row_mass)
    posterior = jnp.where(significant, jnp.exp(scores - log_evidence[None, :]), 0.0).astype(
        jnp.bfloat16
    )
    img_count = lax.axis_size("img")
    slice_width = F // img_count
    slice_start = lax.axis_index("img") * slice_width
    limit_float = term_limit.astype(jnp.float32)
    moved_images = lax.all_to_all(back_images, "img", split_axis=1, concat_axis=0, tiled=True)
    every_post = lax.all_gather(posterior, "img", axis=1, tiled=True)
    focus_all, limit_all = (
        lax.all_gather(defocus, "img", axis=0, tiled=True),
        lax.all_gather(limit_float, "img", axis=0, tiled=True),
    )
    every_post = every_post.reshape(proj_rows, img_count, img_rows)
    moved_images = moved_images.reshape(img_count, img_rows, slice_width)
    part_images = jnp.einsum(
        "jbi,bif->bjf", every_post, moved_images, preferred_element_type=jnp.float32
    )
    part_images = lax.optimization_barrier(part_images.astype(jnp.bfloat16)).astype(jnp.float32)
    sum_images = jnp.sum(part_images, axis=0)
    sum_weights = slice_weight_sums(
        every_post, focus_all, limit_all, slice_start, slice_width, img_count, img_rows
    )
    reconstruction = (sum_images / (sum_weights + 1.0)).astype(jnp.bfloat16)
    every_evidence = lax.all_gather(log_evidence, "img", axis=0, tiled=True)
    blocks = every_evidence.reshape(-1, BLOCK)
    local_blocks = img_rows // BLOCK
    slot_ids = lax.axis_index("img") * local_blocks + jnp.arange(local_blocks, dtype=jnp.int32)
    selector = (block_plan[None, :] == slot_ids[:, None]).astype(jnp.float32)
    own_blocks = jnp.dot(selector, blocks, precision=lax.Precision.HIGHEST)
    return (reconstruction, own_blocks.reshape(img_rows))


def solution(mesh):
    placed = (P("img", None), P("proj", None), P(), P("img"), P("img"), P("img"), P())
    return jax.shard_map(
        shards, mesh=mesh, in_specs=placed, out_specs=(P("proj", "img"), P("img")), check_vma=False
    )
```

profile of v0, /device:TPU:0, one launch (start us, length us, event | category | flops | bytes accessed | tf_op | source)
XLA Modules:
  0.0 115.0 jit_solution(12315028204032979167)
XLA Ops:
  0.7 0.7 broadcast_multiply_fusion.1
  1.3 1.6 %copy.15 = bf16[128,4096]{0,1:T(8,128)(2,1)S(1)} copy(bf16[128,4096]{1,0:T(8,128)(2,1)} %param.7) | data formatting | bytes 2097152 | tf_op args[0]
  2.9 8.5 %fusion.2 = bf16[128,4096]{0,1:T(8,128)(2,1)S(1)} fusion(bf16[128,4096]{0,1:T(8,128)(2,1)S(1)} %copy.15, f32[4096]{0:T(1024)S(1)} %add_multiply_fusion, f32[128]{0:T(128)S(1)} %broadcast_multiply_fusion.1, s32[128]{0:T(128)S(1)} %copy-done.3), kind=kLoop, calls=%fused_computation.8 | loop fusion | flops 3670016 | bytes 2114560 | tf_op jit(solution)/shard_map/convert_element_type | solution.py:24
  11.4 1.3 %copy.16 = bf16[128,4,1024]{2,0,1:T(8,128)(2,1)} copy(bf16[128,4,1024]{0,2,1:T(8,128)(2,1)S(1)} %bitcast.26) | data formatting | bytes 2097152 | tf_op jit(solution)/shard_map/all_to_all | solution.py:70
  12.7 4.3 %all-to-all-start = ((bf16[128,4,1024]{2,0,1:T(8,128)(2,1)}), bf16[128,4,1024]{2,0,1:T(8,128)(2,1)S(1)}, u32[]{:S(2)}, u32[]{:S(2)}) async-start(bf16[128,4,1024]{2,0,1:T(8,128)(2,1)} %copy.16), calls=%async_computation | async-start | bytes 2097152 | tf_op jit(solution)/shard_map/all_to_all | solution.py:70
  17.1 12.5 %convolution_bitcast_fusion = f32[320,128]{1,0:T(8,128)S(1)} fusion(bf16[320,4096]{1,0:T(8,128)(2,1)} %param.8, bf16[128,4096]{0,1:T(8,128)(2,1)S(1)} %copy.15, f32[4096]{0:T(1024)S(1)} %add_multiply_fusion, f32[128]{0:T(128)S(1)} %broadcast_multiply_fusion.1, f32[4096]{0:T(1024)S(1)} %copy-done.5, s32[128]{0:T(128)S(1)} %copy-done.3), kind=kOutput, calls=%fused_computation.19 | convolution fusion | flops 339738624 | bytes 3867648 | tf_op jit(solution)/shard_map/dot_general | solution.py:51
  29.6 8.2 %fusion.32 = (f32[128]{0:T(128)S(1)}, f32[320,128]{1,0:T(8,128)S(1)}) fusion(s32[128]{0:T(128)S(1)} %copy-done.1, s32[320]{0:T(512)S(1)} %iota_add_fusion, f32[320,128]{1,0:T(8,128)S(1)} %convolution_bitcast_fusion, f32[4096]{0:T(1024)S(1)} %add_multiply_fusion, f32[128]{0:T(128)S(1)} %broadcast_multiply_fusion.1, f32[4096]{0:T(1024)S(1)} %copy-done.5, ...), kind=kOutput, calls=%fused_computation.47 | convolution fusion | flops 343351168 | bytes 2985216 | tf_op jit(solution)/shard_map/dot_general | solution.py:52
  37.7 22.6 %pmax.7 = f32[128]{0:T(128)S(1)} all-reduce(f32[128]{0:T(128)S(1)} %get-tuple-element.2), channel_id=1, replica_groups=mesh['img'=4,'proj'=8] {'proj'}, use_global_device_ids=true, to_apply=%region_1.2 | all-reduce | flops 128 | bytes 1024 | tf_op jit(solution)/shard_map/pmax | solution.py:58
  60.3 0.1 fusion.35
  60.5 17.1 %psum.7 = f32[128]{0:T(128)S(1)} all-reduce(f32[128]{0:T(128)S(1)} %fusion.35), channel_id=1, replica_groups=mesh['img'=4,'proj'=8] {'proj'}, use_global_device_ids=true, to_apply=%region_3.4 | all-reduce | flops 128 | bytes 1024 | tf_op jit(solution)/shard_map/psum | solution.py:61
  77.6 0.1 fusion.36
  77.7 5.1 %all-gather.2 = f32[4,1,128]{2,1,0:T(1,128)S(1)} all-gather(f32[1,1,128]{2,1,0:T(1,128)S(1)} %bitcast.27), channel_id=1, replica_groups=mesh['img'=4,'proj'=8] {'img'}, dimensions={0}, use_global_device_ids=true | all-gather | bytes 2560 | tf_op jit(solution)/shard_map/all_gather | solution.py:87
  82.8 0.5 broadcast.84
  83.3 0.7 reduce.3
  84.0 0.2 fusion.37
  84.2 0.6 reshape.74
  84.8 5.3 %all-gather = f32[4,1,128]{2,1,0:T(1,128)S(1)} all-gather(f32[1,1,128]{2,1,0:T(1,128)S(1)} %convert_bitcast_fusion), channel_id=1, replica_groups=mesh['img'=4,'proj'=8] {'img'}, dimensions={0}, use_global_device_ids=true | all-gather | bytes 2560 | tf_op jit(solution)/shard_map/all_gather | solution.py:74
  90.1 5.0 %all-gather.1 = f32[4,1,128]{2,1,0:T(1,128)S(1)} all-gather(f32[1,1,128]{2,1,0:T(1,128)S(1)} %bitcast.30), channel_id=1, replica_groups=mesh['img'=4,'proj'=8] {'img'}, dimensions={0}, use_global_device_ids=true | all-gather | bytes 2560 | tf_op jit(solution)/shard_map/all_gather | solution.py:73
  95.2 6.3 %all_gather.12 = bf16[320,512]{1,0:T(8,128)(2,1)S(1)} all-gather(bf16[320,128]{1,0:T(8,128)(2,1)S(1)} %fusion.36), channel_id=1, replica_groups=mesh['img'=4,'proj'=8] {'img'}, dimensions={1}, use_global_device_ids=true | all-gather | bytes 409600 | tf_op jit(solution)/shard_map/all_gather | solution.py:71
  101.5 9.4 %convolution_convert_fusion = bf16[4,320,1024]{2,1,0:T(8,128)(2,1)} fusion(f32[1024]{0:T(1024)S(1)} %add_multiply_fusion.1, f32[4,128]{1,0:T(4,128)S(1)} %bitcast.29, f32[4,128]{1,0:T(4,128)S(1)} %bitcast.28, f32[1024]{0:T(1024)S(1)} %add_convert_fusion, bf16[320,512]{1,0:T(8,128)(2,1)S(1)} %all_gather.12), kind=kOutput, calls=%fused_computation.14 | convolution fusion | flops 340000768 | bytes 2961408 | tf_op jit(solution)/shard_map/jbi,bif->bjf/dot_general | solution.py:36
  110.9 0.8 convolution_convert_fusion.1
  111.8 0.9 copy-done
  112.7 1.2 %convert_reduce_fusion = (f32[320,1024]{1,0:T(8,128)S(1)}, f32[320,1024]{1,0:T(8,128)S(1)}) fusion(bf16[4,320,1024]{2,1,0:T(8,128)(2,1)S(1)} %copy-done, bf16[4,320,1024]{2,1,0:T(8,128)(2,1)S(1)} %convolution_convert_fusion.1), kind=kLoop, calls=%fused_computation | loop fusion | flops 4587520 | bytes 7864320 | tf_op jit(solution)/shard_map/reduce_sum | solution.py:40
  113.9 1.1 divide_convert_fusion
  (23 shorter events, 0.2 us)
Async XLA Ops:
  0.6 2.3 %copy-start.3 = (s32[128]{0:T(128)S(1)}, s32[128]{0:T(128)}, u32[]{:S(2)}) copy-start(s32[128]{0:T(128)} %param.12) | copy-start | bytes 1540
  11.4 5.6 %copy-start.5 = (f32[4096]{0:T(1024)S(1)}, f32[4096]{0:T(1024)}, u32[]{:S(2)}) copy-start(f32[4096]{0:T(1024)} %param.9) | copy-start | bytes 49156
  12.7 98.2 %all-to-all-start = ((bf16[128,4,1024]{2,0,1:T(8,128)(2,1)}), bf16[128,4,1024]{2,0,1:T(8,128)(2,1)S(1)}, u32[]{:S(2)}, u32[]{:S(2)}) async-start(bf16[128,4,1024]{2,0,1:T(8,128)(2,1)} %copy.16), calls=%async_computation | async-start | bytes 2097152 | tf_op jit(solution)/shard_map/all_to_all | solution.py:70
  17.0 12.5 %copy-start.1 = (s32[128]{0:T(128)S(1)}, s32[128]{0:T(128)}, u32[]{:S(2)}) copy-start(s32[128]{0:T(128)} %param.11) | copy-start | bytes 1540
  17.0 12.5 %copy-start.4 = (bf16[320,4096]{1,0:T(8,128)(2,1)S(1)}, bf16[320,4096]{1,0:T(8,128)(2,1)}, u32[]{:S(2)}) copy-start(bf16[320,4096]{1,0:T(8,128)(2,1)} %param.8) | copy-start | bytes 7864324
  29.6 54.5 %copy-start.6 = (s32[16]{0:T(128)S(1)}, s32[16]{0:T(128)}, u32[]{:S(2)}) copy-start(s32[16]{0:T(128)} %param.13) | copy-start | bytes 196
  29.6 60.6 %copy-start.2 = (f32[128]{0:T(128)S(1)}, f32[128]{0:T(128)}, u32[]{:S(2)}) copy-start(f32[128]{0:T(128)} %param.10) | copy-start | bytes 1540
  110.9 1.7 %copy-start = (bf16[4,320,1024]{2,1,0:T(8,128)(2,1)S(1)}, bf16[4,320,1024]{2,1,0:T(8,128)(2,1)}, u32[]{:S(2)}) copy-start(bf16[4,320,1024]{2,1,0:T(8,128)(2,1)} %convolution_convert_fusion) | copy-start | bytes 7864324
where the time goes:
time: 115 us
  blocking collectives  61.5 us (53%)
  matrix products  31 us (27%)
  other arithmetic  12.4 us (11%)
  local copies, waits for them, and re-layouts  5.05 us (4%)
  starting transfers between devices  4.26 us (4%)
    pmax x1, blocking collectives, shards(): row_peak = lax.pmax(local_peak, 'proj')  22.6 us
    psum x1, blocking collectives, shards(): row_mass = lax.psum(local_mass, 'proj')  17.1 us
    dot_general x1, matrix products, shards(): lax.dot_general(projections, weighted, contract, preferred_element_type=j...  12.5 us
    dot_general x1, matrix products, slice_weight_sums(): jnp.einsum('jbi,bif->bjf', every_post, rebuilt, preferred_element_type=jn...  9.38 us
    convert_element_type x1, other arithmetic, image_terms(): back_images = (keep_mask * contrast * values).astype(jnp.bfloat16)  8.45 us
    dot_general x1, matrix products, shards(): lax.dot_general(proj_sq, weighted_sq, contract, preferred_element_type=jn...  8.17 us
    all_gather x1, blocking collectives, shards(): every_post = lax.all_gather(posterior, 'img', axis=1, tiled=True)  6.34 us
    all_gather x1, blocking collectives, shards(): lax.all_gather(limit_float, 'img', axis=0, tiled=True)  5.29 us
  transfers between devices with their start and end apart: 1, of which 0 were waited for; matrix products, arithmetic and copies ran while one was open for 28% of the time, Pallas kernels for 0%

commit v1 on v0

v1 whole, which is shorter than its diff:
```python
import functools
import math

import jax
import jax.numpy as jnp
from jax import lax
from jax.experimental import pallas as pl
from jax.experimental.pallas import tpu as pltpu
from jax.sharding import PartitionSpec as P

BLOCK = 32
LANES = 128
MESH = pl.DeviceIdType.MESH
SIN_TERMS = [(-1.0) ** k * math.pi ** (2 * k + 1) / math.factorial(2 * k + 1) for k in range(7)]
COS_TERMS = [(-1.0) ** k * math.pi ** (2 * k) / math.factorial(2 * k) for k in range(8)]


def horner(terms, x):
    total = jnp.full_like(x, terms[-1])
    for term in terms[-2::-1]:
        total = total * x + term
    return total


def sincos_turns(turns):
    rest = turns - jnp.floor(turns + 0.5)
    square = rest * rest
    half_sin = rest * horner(SIN_TERMS, square)
    half_cos = horner(COS_TERMS, square)
    return 2.0 * half_sin * half_cos, 1.0 - 2.0 * half_sin * half_sin


def columns_of(row, rows):
    return jnp.broadcast_to(row, (LANES, rows)).T


def kernel(n_img, n_proj, img_hbm, proj_hbm, noise_ref, focus_ref, count_ref, limit_ref, plan_ref,
           rec_ref, ev_ref,
           img, proj, weighted, weighted_sq, moved, contrast, back_img, back_wgt, every_post,
           focus_all, limit_all, terms, every_terms, stats, every_stats, scale_out, every_scale,
           load_sem, small_send, small_recv, img_send, img_recv, post_send, post_recv,
           stat_send, stat_recv, scale_send, scale_recv):
    me = lax.axis_index("img")
    mine = lax.axis_index("proj")
    img_rows, width = img.shape
    proj_rows = proj.shape[0]
    part = width // n_img
    img_peers = [lax.rem(me + k, n_img) for k in range(1, n_img)]
    img_from = [lax.rem(me + n_img - k, n_img) for k in range(1, n_img)]
    proj_peers = [lax.rem(mine + k, n_proj) for k in range(1, n_proj)]

    barrier = pltpu.get_barrier_semaphore()
    for peer in img_peers:
        pl.semaphore_signal(barrier, inc=1, device_id={"img": peer}, device_id_type=MESH)
    for peer in proj_peers:
        pl.semaphore_signal(barrier, inc=1, device_id={"proj": peer}, device_id_type=MESH)
    load_img = pltpu.make_async_copy(img_hbm, img, load_sem.at[0])
    load_proj = pltpu.make_async_copy(proj_hbm, proj, load_sem.at[1])
    load_img.start()
    load_proj.start()

    lane = lax.broadcasted_iota(jnp.int32, (1, LANES), 1).astype(jnp.float32)
    phase = 0.1 / (2.0 * math.pi)
    focus = columns_of(focus_ref[...], img_rows)
    limit = columns_of(limit_ref[...].astype(jnp.float32), img_rows)
    sin0, cos0 = sincos_turns(focus * ((lane + 1.0) / width) + phase)
    sin_d, cos_d = sincos_turns(focus * (LANES / width))

    load_img.wait()
    pl.semaphore_wait(barrier, n_img + n_proj - 2)

    small = []
    moves = []
    for k, peer in enumerate(img_peers):
        for t, (ref, dst) in enumerate(((focus_ref, focus_all), (limit_ref, limit_all))):
            small.append(pltpu.make_async_remote_copy(
                src_ref=ref, dst_ref=dst.at[me], send_sem=small_send.at[t, k],
                recv_sem=small_recv.at[t, k], device_id={"img": peer}, device_id_type=MESH))
    for k, peer in enumerate(img_peers):
        moves.append(pltpu.make_async_remote_copy(
            src_ref=img.at[:, pl.ds(pl.multiple_of(peer * part, LANES), part)],
            dst_ref=moved.at[me], send_sem=img_send.at[k], recv_sem=img_recv.at[k],
            device_id={"img": peer}, device_id_type=MESH))
    for copy in small + moves:
        copy.start()

    def terms_chunk(c, carry):
        sin_v, cos_v = carry
        cols = pl.ds(pl.multiple_of(c * LANES, LANES), LANES)
        term = lane + (c * LANES).astype(jnp.float32)
        kept = jnp.where(term < limit, sin_v, 0.0)
        noisy = kept * noise_ref[:, cols]
        weighted[:, cols] = (noisy * img[:, cols].astype(jnp.float32)).astype(jnp.bfloat16)
        weighted_sq[:, cols] = (noisy * (-0.5 * sin_v)).astype(jnp.bfloat16)
        return sin_v * cos_d + cos_v * sin_d, cos_v * cos_d - sin_v * sin_d

    lax.fori_loop(0, width // LANES, terms_chunk, (sin0, cos0), unroll=2)
    load_proj.wait()

    depth = 512
    contract = (((1,), (1,)), ((), ()))

    def score_chunk(c, total):
        cols = pl.ds(pl.multiple_of(c * depth, depth), depth)
        rows = proj[:, cols]
        total = total + lax.dot_general(rows, weighted[:, cols], contract, preferred_element_type=jnp.float32)
        return total + lax.dot_general(rows * rows, weighted_sq[:, cols], contract,
                                       preferred_element_type=jnp.float32)

    scores = lax.fori_loop(0, width // depth, score_chunk, jnp.zeros((proj_rows, img_rows), jnp.float32))

    orient = lax.broadcasted_iota(jnp.int32, (proj_rows, img_rows), 0) + mine * proj_rows
    significant = orient < count_ref[...]
    peak = jnp.max(jnp.where(significant, scores, -1e30), axis=0, keepdims=True)
    expo = jnp.where(significant, jnp.exp(jnp.where(significant, scores - peak, 0.0)), 0.0)
    mass = jnp.sum(expo, axis=0, keepdims=True)
    stats[0:1, :] = peak
    stats[1:2, :] = mass
    terms[...] = expo.astype(jnp.bfloat16)

    stat_copies = []
    for k, peer in enumerate(proj_peers):
        stat_copies.append(pltpu.make_async_remote_copy(
            src_ref=stats, dst_ref=every_stats.at[mine], send_sem=stat_send.at[k],
            recv_sem=stat_recv.at[k], device_id={"proj": peer}, device_id_type=MESH))
        stat_copies[-1].start()
    post_copies = []
    for k, peer in enumerate(img_peers):
        post_copies.append(pltpu.make_async_remote_copy(
            src_ref=terms, dst_ref=every_terms.at[me], send_sem=post_send.at[k],
            recv_sem=post_recv.at[k], device_id={"img": peer}, device_id_type=MESH))
        post_copies[-1].start()

    for copy in small:
        copy.wait()
    focus_all[me] = focus_ref[...]
    limit_all[me] = limit_ref[...]
    start = (me * part).astype(jnp.float32)
    term0 = lane + start

    def weights_block(b, carry):
        focus_b = columns_of(focus_all[b], img_rows)
        limit_b = columns_of(limit_all[b].astype(jnp.float32), img_rows)
        sin_v, cos_v = sincos_turns(focus_b * ((term0 + 1.0) / width) + phase)
        sin_b, cos_b = sincos_turns(focus_b * (LANES / width))
        rows = pl.ds(pl.multiple_of(b * img_rows, img_rows), img_rows)
        for c in range(part // LANES):
            cols = slice(c * LANES, (c + 1) * LANES)
            kept = jnp.where(term0 + float(c * LANES) < limit_b, sin_v, 0.0)
            contrast[rows, cols] = kept
            back_wgt[rows, cols] = (kept * sin_v).astype(jnp.bfloat16)
            sin_v, cos_v = sin_v * cos_b + cos_v * sin_b, cos_v * cos_b - sin_v * sin_b
        return carry

    lax.fori_loop(0, n_img, weights_block, 0)

    every_stats[mine] = stats[...]
    for copy in stat_copies:
        copy.wait()
    peaks = [every_stats[q, 0:1, :] for q in range(n_proj)]
    top = functools.reduce(jnp.maximum, peaks)
    whole = sum(every_stats[q, 1:2, :] * jnp.exp(peaks[q] - top) for q in range(n_proj))
    evidence = top + jnp.log(whole)
    scale_out[0:1, :] = jnp.exp(peak - evidence)
    scale_out[1:2, :] = evidence
    scale_copies = []
    for k, peer in enumerate(img_peers):
        scale_copies.append(pltpu.make_async_remote_copy(
            src_ref=scale_out, dst_ref=every_scale.at[me], send_sem=scale_send.at[k],
            recv_sem=scale_recv.at[k], device_id={"img": peer}, device_id_type=MESH))
        scale_copies[-1].start()
    every_scale[me] = scale_out[...]

    def take_images(b, pixels):
        rows = pl.ds(pl.multiple_of(b * img_rows, img_rows), img_rows)
        back_img[rows, :] = (contrast[rows, :] * pixels.astype(jnp.float32)).astype(jnp.bfloat16)

    def take_post(b, values):
        cols = pl.ds(pl.multiple_of(b * img_rows, img_rows), img_rows)
        every_post[:, cols] = (values.astype(jnp.float32) * every_scale[b][0:1, :]).astype(jnp.bfloat16)

    take_images(me, img[:, pl.ds(pl.multiple_of(me * part, LANES), part)])
    every_post[:, pl.ds(pl.multiple_of(me * img_rows, img_rows), img_rows)] = (
        expo * every_scale[me][0:1, :]).astype(jnp.bfloat16)
    for k, source in enumerate(img_from):
        moves[k].wait()
        take_images(source, moved[source])
    for k, source in enumerate(img_from):
        post_copies[k].wait()
        scale_copies[k].wait()
        take_post(source, every_terms[source])

    step = min(part, 256)
    posts = every_post[...]
    for c in range(part // step):
        cols = slice(c * step, (c + 1) * step)
        sums = jnp.dot(posts, back_img[:, cols], preferred_element_type=jnp.float32)
        weights = jnp.dot(posts, back_wgt[:, cols], preferred_element_type=jnp.float32)
        rec_ref[:, cols] = (sums / (weights + 1.0)).astype(jnp.bfloat16)

    groups = img_rows // BLOCK
    group = lax.broadcasted_iota(jnp.int32, (1, img_rows), 1) // BLOCK
    placed = jnp.zeros((1, img_rows), jnp.float32)
    for a in range(n_img):
        plan = jnp.zeros((1, img_rows), jnp.int32)
        for g in range(groups):
            plan = jnp.where(group == g, plan_ref[a * groups + g], plan)
        values = every_scale[a][1:2, :]
        for t in range(groups):
            turned, target = values, plan
            if t:
                turned = pltpu.roll(values, t * BLOCK, 1)
                target = pltpu.roll(plan, t * BLOCK, 1)
            placed = placed + jnp.where(target == me * groups + group, turned, 0.0)
    ev_ref[...] = placed


def shards(n_img, n_proj, images, projections, noise_weight, defocus, orient_count, term_limit, block_plan):
    img_rows, width = images.shape
    proj_rows = projections.shape[0]
    part = width // n_img
    vmem = pl.BlockSpec(memory_space=pltpu.VMEM)
    hbm = pl.BlockSpec(memory_space=pl.ANY)
    smem = pl.BlockSpec(memory_space=pltpu.SMEM)
    bf16, f32 = jnp.bfloat16, jnp.float32
    dma = pltpu.SemaphoreType.DMA
    reconstruction, evidence = pl.pallas_call(
        functools.partial(kernel, n_img, n_proj),
        out_shape=(jax.ShapeDtypeStruct((proj_rows, part), bf16), jax.ShapeDtypeStruct((1, img_rows), f32)),
        in_specs=[hbm, hbm, vmem, vmem, vmem, vmem, smem],
        out_specs=(vmem, vmem),
        scratch_shapes=[
            pltpu.VMEM((img_rows, width), bf16),
            pltpu.VMEM((proj_rows, width), bf16),
            pltpu.VMEM((img_rows, width), bf16),
            pltpu.VMEM((img_rows, width), bf16),
            pltpu.VMEM((n_img, img_rows, part), bf16),
            pltpu.VMEM((n_img * img_rows, part), f32),
            pltpu.VMEM((n_img * img_rows, part), bf16),
            pltpu.VMEM((n_img * img_rows, part), bf16),
            pltpu.VMEM((proj_rows, n_img * img_rows), bf16),
            pltpu.VMEM((n_img, 1, img_rows), f32),
            pltpu.VMEM((n_img, 1, img_rows), jnp.int32),
            pltpu.VMEM((proj_rows, img_rows), bf16),
            pltpu.VMEM((n_img, proj_rows, img_rows), bf16),
            pltpu.VMEM((2, img_rows), f32),
            pltpu.VMEM((n_proj, 2, img_rows), f32),
            pltpu.VMEM((2, img_rows), f32),
            pltpu.VMEM((n_img, 2, img_rows), f32),
            dma((2,)),
            dma((2, n_img)), dma((2, n_img)),
            dma((n_img,)), dma((n_img,)),
            dma((n_img,)), dma((n_img,)),
            dma((n_proj,)), dma((n_proj,)),
            dma((n_img,)), dma((n_img,)),
        ],
        compiler_params=pltpu.CompilerParams(
            collective_id=0, has_side_effects=True, vmem_limit_bytes=40 * 1024 * 1024),
    )(images, projections, noise_weight.reshape(1, -1), defocus.reshape(1, -1), orient_count.reshape(1, -1),
      term_limit.reshape(1, -1), block_plan)
    return reconstruction, evidence.reshape(-1)


def solution(mesh):
    n_img, n_proj = mesh.shape["img"], mesh.shape["proj"]
    placed = (P("img", None), P("proj", None), P(), P("img"), P("img"), P("img"), P())
    return jax.shard_map(
        functools.partial(shards, n_img, n_proj), mesh=mesh, in_specs=placed,
        out_specs=(P("proj", "img"), P("img")), check_vma=False,
    )
```

time: 115 us -> 33.3 us (0.29)
  blocking collectives: 61.5 us -> 0 us
  matrix products: 31 us -> 0 us
  Pallas kernels: 0 us -> 24.8 us
  other arithmetic: 12.4 us -> 0 us
  starting transfers between devices: 4.26 us -> 0 us
  local copies, waits for them, and re-layouts: 5.05 us -> 7.64 us
    dot_general x5 -> x0, matrix products: 31 us -> none  [the longest x1 12.5 us: shards(): lax.dot_general(projections, weighted, contract, preferred_element_type=j...]
    pallas_call x0 -> x1, Pallas kernels: none -> 24.8 us  [shards(): pl.pallas_call(functools.partial(kernel, n_img, n_proj), out_shape=(jax.S...]
    pmax x1 -> x0, blocking collectives: 22.6 us -> none  [shards(): row_peak = lax.pmax(local_peak, 'proj')]
    all_gather x4 -> x0, blocking collectives: 21.7 us -> none  [the longest x1 6.34 us: shards(): every_post = lax.all_gather(posterior, 'img', axis=1, tiled=True)]
    psum x1 -> x0, blocking collectives: 17.1 us -> none  [shards(): row_mass = lax.psum(local_mass, 'proj')]
    convert_element_type x4 -> x0, other arithmetic: 9.63 us -> none  [the longest x1 8.45 us: image_terms(): back_images = (keep_mask * contrast * values).astype(jnp.bfloat16)]
    unnamed x15 -> x16, local copies, waits for them, and re-layouts: 2.55 us -> 7.64 us
    all_to_all x1 -> x0, starting transfers between devices: 4.26 us -> none  [shards(): lax.all_to_all(back_images, 'img', split_axis=1, concat_axis=0, tiled=True)]
  transfers between devices with their start and end apart: 1 -> 0, of which waited for: 0 -> 0; matrix products, arithmetic and copies ran while one was open for 28% -> 0% of each run, Pallas kernels for 0% -> 0%
where the time goes in v1:
time: 33.3 us; the launch traced here: 33 us
  Pallas kernels  24.8 us (74%)
  local copies, waits for them, and re-layouts  7.64 us (23%)
  between operations  0.66 us (2%)
    pallas_call x1, Pallas kernels, shards(): pl.pallas_call(functools.partial(kernel, n_img, n_proj), out_shape=(jax.S...  24.8 us
    unnamed x16, local copies, waits for them, and re-layouts  7.64 us

profile of v1, /device:TPU:0, one launch (start us, length us, event | category | flops | bytes accessed | tf_op | source)
XLA Modules:
  0.0 33.0 jit_solution(5673988448185382330)
XLA Ops:
  0.6 0.0 copy-start
  0.6 1.7 %copy-done = bf16[320,4096]{1,0:T(8,128)(2,1)S(1)} copy-done((bf16[320,4096]{1,0:T(8,128)(2,1)S(1)}, bf16[320,4096]{1,0:T(8,128)(2,1)}, u32[]{:S(2)}) %copy-start) | copy-done | bytes 2621464
  2.4 0.0 copy-start.1
  2.4 1.2 %copy-done.1 = bf16[128,4096]{1,0:T(8,128)(2,1)S(1)} copy-done((bf16[128,4096]{1,0:T(8,128)(2,1)S(1)}, bf16[128,4096]{1,0:T(8,128)(2,1)}, u32[]{:S(2)}) %copy-start.1) | copy-done | bytes 1048600
  3.6 0.0 copy-start.2
  3.6 0.7 %copy-done.2 = f32[4096]{0:T(1024)S(1)} copy-done((f32[4096]{0:T(1024)S(1)}, f32[4096]{0:T(1024)}, u32[]{:S(2)}) %copy-start.2) | copy-done | bytes 16408
  4.3 0.0 copy-start.3
  4.3 0.7 %copy-done.3 = f32[128]{0:T(128)S(1)} copy-done((f32[128]{0:T(128)S(1)}, f32[128]{0:T(128)}, u32[]{:S(2)}) %copy-start.3) | copy-done | bytes 536
  5.0 0.0 copy-start.4
  5.0 0.7 %copy-done.4 = s32[128]{0:T(128)S(1)} copy-done((s32[128]{0:T(128)S(1)}, s32[128]{0:T(128)}, u32[]{:S(2)}) %copy-start.4) | copy-done | bytes 536
  5.6 0.0 copy-start.5
  5.6 0.7 %copy-done.5 = s32[128]{0:T(128)S(1)} copy-done((s32[128]{0:T(128)S(1)}, s32[128]{0:T(128)}, u32[]{:S(2)}) %copy-start.5) | copy-done | bytes 536
  6.3 0.0 copy-start.6
  6.3 0.7 %copy-done.6 = s32[16]{0:T(128)S(1)} copy-done((s32[16]{0:T(128)S(1)}, s32[16]{0:T(128)}, u32[]{:S(2)}) %copy-start.6) | copy-done | bytes 88
  6.9 24.8 %shard_map.86 = (bf16[320,1024]{1,0:T(8,128)(2,1)S(1)}, f32[1,128]{1,0:T(1,128)S(1)}) custom-call(bf16[128,4096]{1,0:T(8,128)(2,1)S(1)} %copy-done.1, bf16[320,4096]{1,0:T(8,128)(2,1)S(1)} %copy-done, f32[1,4096]{1,0:T(1,128)S(1)} %bitcast.5, f32[1,128]{1,0:T(1,128)S(1)} %bitcast.6, s32[1,128]{1,0:T(1,128)S(1)} %bitcast.7, s32[1,128]{1,0:T(1,128)S(1)} %bitcast.8, ...), custom_call_target="tpu_custom_call" | custom-call | tf_op jit(solution)/shard_map/pallas_call | solution.py:227
  31.7 0.8 %copy.11 = bf16[320,1024]{1,0:T(8,128)(2,1)} copy(bf16[320,1024]{1,0:T(8,128)(2,1)S(1)} %get-tuple-element.8) | data formatting | bytes 1310720
  32.5 0.5 %copy.12 = f32[128]{0:T(128)} copy(f32[128]{0:T(128)S(1)} %bitcast.9) | data formatting | bytes 1024
Async XLA Ops:
  0.6 1.7 %copy-start = (bf16[320,4096]{1,0:T(8,128)(2,1)S(1)}, bf16[320,4096]{1,0:T(8,128)(2,1)}, u32[]{:S(2)}) copy-start(bf16[320,4096]{1,0:T(8,128)(2,1)} %proj_hbm.1) | copy-start | bytes 7864324
  2.4 1.2 %copy-start.1 = (bf16[128,4096]{1,0:T(8,128)(2,1)S(1)}, bf16[128,4096]{1,0:T(8,128)(2,1)}, u32[]{:S(2)}) copy-start(bf16[128,4096]{1,0:T(8,128)(2,1)} %img_hbm.1) | copy-start | bytes 3145732
  3.6 0.7 %copy-start.2 = (f32[4096]{0:T(1024)S(1)}, f32[4096]{0:T(1024)}, u32[]{:S(2)}) copy-start(f32[4096]{0:T(1024)} %param.9) | copy-start | bytes 49156
  4.3 0.7 %copy-start.3 = (f32[128]{0:T(128)S(1)}, f32[128]{0:T(128)}, u32[]{:S(2)}) copy-start(f32[128]{0:T(128)} %param.10) | copy-start | bytes 1540
  5.0 0.7 %copy-start.4 = (s32[128]{0:T(128)S(1)}, s32[128]{0:T(128)}, u32[]{:S(2)}) copy-start(s32[128]{0:T(128)} %param.11) | copy-start | bytes 1540
  5.6 0.7 %copy-start.5 = (s32[128]{0:T(128)S(1)}, s32[128]{0:T(128)}, u32[]{:S(2)}) copy-start(s32[128]{0:T(128)} %param.12) | copy-start | bytes 1540
  6.3 0.7 %copy-start.6 = (s32[16]{0:T(128)S(1)}, s32[16]{0:T(128)}, u32[]{:S(2)}) copy-start(s32[16]{0:T(128)} %plan_ref.1) | copy-start | bytes 196

commit v2 on v1

--- a/solution.py
+++ b/solution.py
@@ -34,9 +34,9 @@
     return jnp.broadcast_to(row, (LANES, rows)).T
 
 
-def kernel(n_img, n_proj, img_hbm, proj_hbm, noise_ref, focus_ref, count_ref, limit_ref, plan_ref,
+def kernel(n_img, n_proj, img_hbm, proj_hbm, noise_hbm, focus_hbm, count_hbm, limit_hbm, plan_hbm,
            rec_ref, ev_ref,
-           img, proj, weighted, weighted_sq, moved, contrast, back_img, back_wgt, every_post,
+           img, proj, noise_ref, focus_ref, count_ref, limit_ref, plan_ref, weighted, weighted_sq, moved, contrast, back_img, back_wgt, every_post,
            focus_all, limit_all, terms, every_terms, stats, every_stats, scale_out, every_scale,
            load_sem, small_send, small_recv, img_send, img_recv, post_send, post_recv,
            stat_send, stat_recv, scale_send, scale_recv):
@@ -54,10 +54,14 @@
         pl.semaphore_signal(barrier, inc=1, device_id={"img": peer}, device_id_type=MESH)
     for peer in proj_peers:
         pl.semaphore_signal(barrier, inc=1, device_id={"proj": peer}, device_id_type=MESH)
-    load_img = pltpu.make_async_copy(img_hbm, img, load_sem.at[0])
-    load_proj = pltpu.make_async_copy(proj_hbm, proj, load_sem.at[1])
-    load_img.start()
-    load_proj.start()
+    sources = (focus_hbm, limit_hbm, img_hbm, noise_hbm, count_hbm, plan_hbm, proj_hbm)
+    targets = (focus_ref, limit_ref, img, noise_ref, count_ref, plan_ref, proj)
+    loads = [pltpu.make_async_copy(source, target, load_sem.at[n])
+             for n, (source, target) in enumerate(zip(sources, targets))]
+    for load in loads:
+        load.start()
+    loads[0].wait()
+    loads[1].wait()
 
     lane = lax.broadcasted_iota(jnp.int32, (1, LANES), 1).astype(jnp.float32)
     phase = 0.1 / (2.0 * math.pi)
@@ -66,7 +70,8 @@
     sin0, cos0 = sincos_turns(focus * ((lane + 1.0) / width) + phase)
     sin_d, cos_d = sincos_turns(focus * (LANES / width))
 
-    load_img.wait()
+    for load in loads[2:6]:
+        load.wait()
     pl.semaphore_wait(barrier, n_img + n_proj - 2)
 
     small = []
@@ -95,7 +100,7 @@
         return sin_v * cos_d + cos_v * sin_d, cos_v * cos_d - sin_v * sin_d
 
     lax.fori_loop(0, width // LANES, terms_chunk, (sin0, cos0), unroll=2)
-    load_proj.wait()
+    loads[6].wait()
 
     depth = 512
     contract = (((1,), (1,)), ((), ()))
@@ -221,17 +226,21 @@
     part = width // n_img
     vmem = pl.BlockSpec(memory_space=pltpu.VMEM)
     hbm = pl.BlockSpec(memory_space=pl.ANY)
-    smem = pl.BlockSpec(memory_space=pltpu.SMEM)
     bf16, f32 = jnp.bfloat16, jnp.float32
     dma = pltpu.SemaphoreType.DMA
     reconstruction, evidence = pl.pallas_call(
         functools.partial(kernel, n_img, n_proj),
         out_shape=(jax.ShapeDtypeStruct((proj_rows, part), bf16), jax.ShapeDtypeStruct((1, img_rows), f32)),
-        in_specs=[hbm, hbm, vmem, vmem, vmem, vmem, smem],
+        in_specs=[hbm] * 7,
         out_specs=(vmem, vmem),
         scratch_shapes=[
             pltpu.VMEM((img_rows, width), bf16),
             pltpu.VMEM((proj_rows, width), bf16),
+            pltpu.VMEM((1, width), f32),
+            pltpu.VMEM((1, img_rows), f32),
+            pltpu.VMEM((1, img_rows), jnp.int32),
+            pltpu.VMEM((1, img_rows), jnp.int32),
+            pltpu.SMEM(block_plan.shape, jnp.int32),
             pltpu.VMEM((img_rows, width), bf16),
             pltpu.VMEM((img_rows, width), bf16),
             pltpu.VMEM((n_img, img_rows, part), bf16),
@@ -247,7 +256,7 @@
             pltpu.VMEM((n_proj, 2, img_rows), f32),
             pltpu.VMEM((2, img_rows), f32),
             pltpu.VMEM((n_img, 2, img_rows), f32),
-            dma((2,)),
+            dma((7,)),
             dma((2, n_img)), dma((2, n_img)),
             dma((n_img,)), dma((n_img,)),
             dma((n_img,)), dma((n_img,)),
@@ -255,7 +264,7 @@
             dma((n_img,)), dma((n_img,)),
         ],
         compiler_params=pltpu.CompilerParams(
-            collective_id=0, has_side_effects=True, vmem_limit_bytes=40 * 1024 * 1024),
+            collective_id=0, has_side_effects=True, vmem_limit_bytes=62 * 1024 * 1024),
     )(images, projections, noise_weight.reshape(1, -1), defocus.reshape(1, -1), orient_count.reshape(1, -1),
       term_limit.reshape(1, -1), block_plan)
     return reconstruction, evidence.reshape(-1)

time: 33.3 us -> 29.1 us (0.87)
  local copies, waits for them, and re-layouts: 7.64 us -> 3.13 us
    unnamed x16 -> x2, local copies, waits for them, and re-layouts: 7.64 us -> 3.13 us
    pallas_call x1, Pallas kernels: 24.8 us -> 25.1 us  [shards(): pl.pallas_call(functools.partial(kernel, n_img, n_proj), out_shape=(jax.S...]
where the time goes in v2:
time: 29.1 us; the launch traced here: 28.9 us
  Pallas kernels  25.1 us (86%)
  local copies, waits for them, and re-layouts  3.13 us (11%)
  between operations  0.64 us (2%)
    pallas_call x1, Pallas kernels, shards(): pl.pallas_call(functools.partial(kernel, n_img, n_proj), out_shape=(jax.S...  25.1 us
    unnamed x2, local copies, waits for them, and re-layouts  3.13 us

profile of v2, /device:TPU:0, one launch (start us, length us, event | category | flops | bytes accessed | tf_op | source)
XLA Modules:
  0.0 28.9 jit_solution(12517813918677529483)
XLA Ops:
  0.6 25.1 %shard_map.86 = (bf16[320,1024]{1,0:T(8,128)(2,1)}, f32[1,128]{1,0:T(1,128)}) custom-call(bf16[128,4096]{1,0:T(8,128)(2,1)} %img_hbm.1, bf16[320,4096]{1,0:T(8,128)(2,1)} %proj_hbm.1, f32[1,4096]{1,0:T(1,128)} %bitcast.5, f32[1,128]{1,0:T(1,128)} %bitcast.6, s32[1,128]{1,0:T(1,128)} %bitcast.7, s32[1,128]{1,0:T(1,128)} %bitcast.8, s32[16]{0:T(128)} %plan_hbm.1), custom_call_target="tpu_custom_call" | custom-call | tf_op jit(solution)/shard_map/pallas_call | solution.py:231
  25.8 2.0 %copy.11 = bf16[320,1024]{1,0:T(8,128)(2,1)} copy(bf16[320,1024]{1,0:T(8,128)(2,1)} %get-tuple-element.8) | data formatting | bytes 1310720
  27.7 1.2 %copy.12 = f32[128]{0:T(128)} copy(f32[128]{0:T(128)} %bitcast.9) | data formatting | bytes 1024

commit v3 on v2

--- a/solution.py
+++ b/solution.py
@@ -9,6 +9,7 @@
 from jax.sharding import PartitionSpec as P
 
 BLOCK = 32
+PIECES = 2
 LANES = 128
 MESH = pl.DeviceIdType.MESH
 SIN_TERMS = [(-1.0) ** k * math.pi ** (2 * k + 1) / math.factorial(2 * k + 1) for k in range(7)]
@@ -38,15 +39,21 @@
            rec_ref, ev_ref,
            img, proj, noise_ref, focus_ref, count_ref, limit_ref, plan_ref, weighted, weighted_sq, moved, contrast, back_img, back_wgt, every_post,
            focus_all, limit_all, terms, every_terms, stats, every_stats, scale_out, every_scale,
-           load_sem, small_send, small_recv, img_send, img_recv, post_send, post_recv,
+           load_sem, small_send, small_recv, img_send, img_recv, pass_send, pass_recv, post_send, post_recv,
            stat_send, stat_recv, scale_send, scale_recv):
     me = lax.axis_index("img")
     mine = lax.axis_index("proj")
     img_rows, width = img.shape
     proj_rows = proj.shape[0]
     part = width // n_img
-    img_peers = [lax.rem(me + k, n_img) for k in range(1, n_img)]
-    img_from = [lax.rem(me + n_img - k, n_img) for k in range(1, n_img)]
+    chips = n_img // 2
+    row_y, core = me // 2, lax.rem(me, 2)
+    offsets = [(dy, dc) for dy in range(chips - 1, -1, -1) for dc in range(2) if dy or dc]
+    img_peers = [lax.rem(row_y + dy, chips) * 2 + lax.rem(core + dc, 2) for dy, dc in offsets]
+    img_from = [lax.rem(row_y + chips - dy, chips) * 2 + lax.rem(core + dc, 2) for dy, dc in offsets]
+    side = lax.rem(mine, 2)
+    beside = mine + 1 - 2 * side
+    piece = img_rows // 2 // PIECES
     proj_peers = [lax.rem(mine + k, n_proj) for k in range(1, n_proj)]
 
     barrier = pltpu.get_barrier_semaphore()
@@ -72,22 +79,6 @@
 
     for load in loads[2:6]:
         load.wait()
-    pl.semaphore_wait(barrier, n_img + n_proj - 2)
-
-    small = []
-    moves = []
-    for k, peer in enumerate(img_peers):
-        for t, (ref, dst) in enumerate(((focus_ref, focus_all), (limit_ref, limit_all))):
-            small.append(pltpu.make_async_remote_copy(
-                src_ref=ref, dst_ref=dst.at[me], send_sem=small_send.at[t, k],
-                recv_sem=small_recv.at[t, k], device_id={"img": peer}, device_id_type=MESH))
-    for k, peer in enumerate(img_peers):
-        moves.append(pltpu.make_async_remote_copy(
-            src_ref=img.at[:, pl.ds(pl.multiple_of(peer * part, LANES), part)],
-            dst_ref=moved.at[me], send_sem=img_send.at[k], recv_sem=img_recv.at[k],
-            device_id={"img": peer}, device_id_type=MESH))
-    for copy in small + moves:
-        copy.start()
 
     def terms_chunk(c, carry):
         sin_v, cos_v = carry
@@ -123,12 +114,37 @@
     stats[1:2, :] = mass
     terms[...] = expo.astype(jnp.bfloat16)
 
+    pl.semaphore_wait(barrier, n_img + n_proj - 2)
+
+    small = []
+    for k, peer in enumerate(img_peers):
+        for t, (ref, dst) in enumerate(((focus_ref, focus_all), (limit_ref, limit_all))):
+            small.append(pltpu.make_async_remote_copy(
+                src_ref=ref, dst_ref=dst.at[me], send_sem=small_send.at[t, k],
+                recv_sem=small_recv.at[t, k], device_id={"img": peer}, device_id_type=MESH))
+            small[-1].start()
     stat_copies = []
     for k, peer in enumerate(proj_peers):
         stat_copies.append(pltpu.make_async_remote_copy(
             src_ref=stats, dst_ref=every_stats.at[mine], send_sem=stat_send.at[k],
             recv_sem=stat_recv.at[k], device_id={"proj": peer}, device_id_type=MESH))
         stat_copies[-1].start()
+    moves = []
+    for k, peer in enumerate(img_peers):
+        slab = pl.ds(pl.multiple_of(peer * part, LANES), part)
+        if offsets[k][0]:
+            for n in range(PIECES):
+                rows = pl.ds(pl.multiple_of((side * PIECES + n) * piece, piece), piece)
+                moves.append((k, n, pltpu.make_async_remote_copy(
+                    src_ref=img.at[rows, slab], dst_ref=moved.at[me, rows, :], send_sem=img_send.at[k, n],
+                    recv_sem=img_recv.at[k, n], device_id={"img": peer}, device_id_type=MESH)))
+        else:
+            near = pltpu.make_async_remote_copy(
+                src_ref=img.at[:, slab], dst_ref=moved.at[me], send_sem=img_send.at[k, 0],
+                recv_sem=img_recv.at[k, 0], device_id={"img": peer}, device_id_type=MESH)
+    for _, _, copy in moves:
+        copy.start()
+    near.start()
     post_copies = []
     for k, peer in enumerate(img_peers):
         post_copies.append(pltpu.make_async_remote_copy(
@@ -187,13 +203,24 @@
     take_images(me, img[:, pl.ds(pl.multiple_of(me * part, LANES), part)])
     every_post[:, pl.ds(pl.multiple_of(me * img_rows, img_rows), img_rows)] = (
         expo * every_scale[me][0:1, :]).astype(jnp.bfloat16)
-    for k, source in enumerate(img_from):
-        moves[k].wait()
-        take_images(source, moved[source])
+    near.wait()
+    take_images(img_from[-1], moved[img_from[-1]])
+    passed = []
+    for k, n, copy in moves:
+        copy.wait()
+        held = moved.at[img_from[k], pl.ds(pl.multiple_of((side * PIECES + n) * piece, piece), piece), :]
+        passed.append(pltpu.make_async_remote_copy(
+            src_ref=held, dst_ref=held, send_sem=pass_send.at[k, n], recv_sem=pass_recv.at[k, n],
+            device_id={"proj": beside}, device_id_type=MESH))
+        passed[-1].start()
     for k, source in enumerate(img_from):
         post_copies[k].wait()
         scale_copies[k].wait()
         take_post(source, every_terms[source])
+    for copy in passed:
+        copy.wait()
+    for source in img_from[:-1]:
+        take_images(source, moved[source])
 
     step = min(part, 256)
     posts = every_post[...]
@@ -258,7 +285,8 @@
             pltpu.VMEM((n_img, 2, img_rows), f32),
             dma((7,)),
             dma((2, n_img)), dma((2, n_img)),
-            dma((n_img,)), dma((n_img,)),
+            dma((n_img, PIECES)), dma((n_img, PIECES)),
+            dma((n_img, PIECES)), dma((n_img, PIECES)),
             dma((n_img,)), dma((n_img,)),
             dma((n_proj,)), dma((n_proj,)),
             dma((n_img,)), dma((n_img,)),

time: 29.1 us -> 26.4 us (0.907)
  Pallas kernels: 25.1 us -> 22.4 us
    pallas_call x1, Pallas kernels: 25.1 us -> 22.4 us  [shards(): pl.pallas_call(functools.partial(kernel, n_img, n_proj), out_shape=(jax.S...]
where the time goes in v3:
time: 26.4 us; the launch traced here: 26.2 us
  Pallas kernels  22.4 us (85%)
  local copies, waits for them, and re-layouts  3.13 us (12%)
  between operations  0.64 us (2%)
    pallas_call x1, Pallas kernels, shards(): pl.pallas_call(functools.partial(kernel, n_img, n_proj), out_shape=(jax.S...  22.4 us
    unnamed x2, local copies, waits for them, and re-layouts  3.13 us

profile of v3, /device:TPU:0, one launch (start us, length us, event | category | flops | bytes accessed | tf_op | source)
XLA Modules:
  0.0 26.2 jit_solution(3945047810210811608)
XLA Ops:
  0.6 22.4 %shard_map.86 = (bf16[320,1024]{1,0:T(8,128)(2,1)}, f32[1,128]{1,0:T(1,128)}) custom-call(bf16[128,4096]{1,0:T(8,128)(2,1)} %img_hbm.1, bf16[320,4096]{1,0:T(8,128)(2,1)} %proj_hbm.1, f32[1,4096]{1,0:T(1,128)} %bitcast.5, f32[1,128]{1,0:T(1,128)} %bitcast.6, s32[1,128]{1,0:T(1,128)} %bitcast.7, s32[1,128]{1,0:T(1,128)} %bitcast.8, s32[16]{0:T(128)} %plan_hbm.1), custom_call_target="tpu_custom_call" | custom-call | tf_op jit(solution)/shard_map/pallas_call | solution.py:258
  23.1 2.0 %copy.11 = bf16[320,1024]{1,0:T(8,128)(2,1)} copy(bf16[320,1024]{1,0:T(8,128)(2,1)} %get-tuple-element.8) | data formatting | bytes 1310720
  25.0 1.2 %copy.12 = f32[128]{0:T(128)} copy(f32[128]{0:T(128)} %bitcast.9) | data formatting | bytes 1024

commit v4 on v3

--- a/solution.py
+++ b/solution.py
@@ -150,7 +150,8 @@
         post_copies.append(pltpu.make_async_remote_copy(
             src_ref=terms, dst_ref=every_terms.at[me], send_sem=post_send.at[k],
             recv_sem=post_recv.at[k], device_id={"img": peer}, device_id_type=MESH))
-        post_copies[-1].start()
+        if offsets[k] == (0, 1) or not offsets[k][1]:
+            post_copies[-1].start()
 
     for copy in small:
         copy.wait()
@@ -215,6 +216,12 @@
         passed[-1].start()
     for k, source in enumerate(img_from):
         post_copies[k].wait()
+        if not offsets[k][1]:
+            held = every_terms.at[source]
+            post_copies[k + 1] = pltpu.make_async_remote_copy(
+                src_ref=held, dst_ref=held, send_sem=post_send.at[k + 1], recv_sem=post_recv.at[k + 1],
+                device_id={"img": img_peers[-1]}, device_id_type=MESH)
+            post_copies[k + 1].start()
         scale_copies[k].wait()
         take_post(source, every_terms[source])
     for copy in passed:

time: 26.4 us -> 26.4 us (level)
  no operation moved by 1% of the time
where the time goes in v4:
time: 26.4 us; the launch traced here: 26.2 us
  Pallas kernels  22.4 us (85%)
  local copies, waits for them, and re-layouts  3.13 us (12%)
  between operations  0.64 us (2%)
    pallas_call x1, Pallas kernels, shards(): pl.pallas_call(functools.partial(kernel, n_img, n_proj), out_shape=(jax.S...  22.4 us
    unnamed x2, local copies, waits for them, and re-layouts  3.13 us

profile of v4, /device:TPU:0, one launch (start us, length us, event | category | flops | bytes accessed | tf_op | source)
XLA Modules:
  0.0 26.2 jit_solution(17970020152602561373)
XLA Ops:
  0.6 22.4 %shard_map.86 = (bf16[320,1024]{1,0:T(8,128)(2,1)}, f32[1,128]{1,0:T(1,128)}) custom-call(bf16[128,4096]{1,0:T(8,128)(2,1)} %img_hbm.1, bf16[320,4096]{1,0:T(8,128)(2,1)} %proj_hbm.1, f32[1,4096]{1,0:T(1,128)} %bitcast.5, f32[1,128]{1,0:T(1,128)} %bitcast.6, s32[1,128]{1,0:T(1,128)} %bitcast.7, s32[1,128]{1,0:T(1,128)} %bitcast.8, s32[16]{0:T(128)} %plan_hbm.1), custom_call_target="tpu_custom_call" | custom-call | tf_op jit(solution)/shard_map/pallas_call | solution.py:265
  23.1 2.0 %copy.11 = bf16[320,1024]{1,0:T(8,128)(2,1)} copy(bf16[320,1024]{1,0:T(8,128)(2,1)} %get-tuple-element.8) | data formatting | bytes 1310720
  25.0 1.2 %copy.12 = f32[128]{0:T(128)} copy(f32[128]{0:T(128)} %bitcast.9) | data formatting | bytes 1024
